TPU v7x, 128 devices: a whole 4x4x4 slice. The times are simulated.
128 devices in a mesh: seq: 16 (over y_hi, z, core), tp: 8 (over x, y_lo).
Axes of the slice: x: 4, y: 4 (y_hi: 2, y_lo: 2; y = y_hi * 2 + y_lo), z: 4, core: 2. Of those that a mesh axis runs over, the one named last changes fastest.
Arguments:
- streams: bfloat16 [8192, 4, 4096], P('seq', None, 'tp'), may hold values from -6 to 6
- doc_ids: int32 [8192], P('seq'), may hold values from 0 to 3, never falling along the last dimension, each value on 1 to 4096 neighbouring positions
- mix_weight: float32 [4, 4096, 24], P(None, 'tp'), may hold values from -0.046875 to 0.046875
- mix_bias: float32 [24], replicated, may hold values from -1 to 1
- attn_gain: float32 [4096], replicated, may hold values from 0.1 to 1.9
- w_qkv: bfloat16 [4096, 3, 4096], P(None, None, 'tp'), may hold values from -1 to 1
- w_out: bfloat16 [4096, 4096], P('tp'), may hold values from -0.5 to 0.5
Outputs:
- new_streams: bfloat16 [8192, 4, 4096], P('seq', None, 'tp')
Inputs may be any that keep to these rules, and one draw needn't show every extreme that they name: doc_ids never fall along the sequence; each of the 4 documents has 1 to 4096 positions, and the longest has exactly 4096.
All inputs are finite; a program needn't handle non-finite values.
Results may differ from a plain program's by a relative error of at most 0.014.
The roundings to bfloat16 on the way count: a program that leaves them out, or rounds other values in their place, can miss the bound.
Values may be sent and summed in bfloat16 or wider, within the bound.
A program may use at most 256 MiB of HBM per device.

v0:
```python
import jax
import jax.numpy as jnp
from jax import lax
from jax.sharding import Mesh
from jax.sharding import PartitionSpec as P

D = 4096
HEAD_DIM = 128
STREAMS = 4
BALANCE_ROUNDS = 20
TP = ("tp_0", "tp_1")


masked_score = -1e30
norm_eps = 1e-06


def from_everyone(x, axis):
    copies = jnp.broadcast_to(x, (lax.axis_size(axis), *x.shape))
    return lax.all_to_all(copies, axis, split_axis=0, concat_axis=0, tiled=True)


def taken_together(x, axis):
    return from_everyone(x, axis).sum(axis=0)


def packed_total(arrays, axis):
    vector, at, done = (jnp.concatenate([a.reshape(-1) for a in arrays]), 0, [])
    subtotal = taken_together(vector, axis)
    for a in arrays:
        done.append(subtotal[at : at + a.size].reshape(a.shape))
        at += a.size
    return tuple(done)


def gathered_by_axis(x, axes, dim):
    if not axes:
        return x
    nearer = lax.all_gather(x, axes[-1], axis=dim, tiled=True)
    return gathered_by_axis(nearer, axes[:-1], dim)


def summed_rows(terms, axes):
    subtotal = terms.astype(jnp.bfloat16)
    for axis in axes:
        subtotal = lax.psum_scatter(subtotal, axis, scatter_dimension=0, tiled=True)
    return subtotal.astype(jnp.float32)


def doubly_stochastic(mixing_matrix):

    def balance_round(round_index, running_matrix):
        running_matrix = running_matrix / jnp.sum(running_matrix, axis=2, keepdims=True)
        return running_matrix / jnp.sum(running_matrix, axis=1, keepdims=True)

    return lax.fori_loop(0, BALANCE_ROUNDS, balance_round, mixing_matrix)


def coefficients(squares, partial_logits, mix_bias):
    root_mean = jnp.sqrt(squares / (STREAMS * D) + norm_eps)
    coef_logits = partial_logits / root_mean[:, None] + mix_bias
    input_weights = jax.nn.sigmoid(coef_logits[:, :STREAMS])
    output_weights = 2.0 * jax.nn.sigmoid(coef_logits[:, STREAMS : 2 * STREAMS])
    unnormalized_mixing = jnp.exp(coef_logits[:, 2 * STREAMS :]).reshape(-1, STREAMS, STREAMS)
    return (input_weights, output_weights, doubly_stochastic(unnormalized_mixing))


def attend(running, queries, keys_values, key_doc, query_pos, query_doc):
    top_score, denominator, weighted = running
    key_count = keys_values.shape[0]
    heads_local = queries.shape[1]
    keys = keys_values[:, 0].reshape(key_count, heads_local, HEAD_DIM)
    values = keys_values[:, 1].reshape(key_count, heads_local, HEAD_DIM)
    scores = jnp.einsum(
        "qhd,khd->qhk", queries, keys, preferred_element_type=jnp.float32
    ) * HEAD_DIM ** (-0.5)
    key_pos = jnp.arange(key_count, dtype=jnp.int32)
    allowed = ((key_pos[None, :] <= query_pos[:, None]) & (key_doc[None, :] == query_doc[:, None]))[
        :, None, :
    ]
    scores = jnp.where(allowed, scores, masked_score)
    new_top = jnp.maximum(top_score, jnp.max(scores, axis=2))
    weights = jnp.where(allowed, jnp.exp(scores - new_top[:, :, None]), 0.0)
    denominator = jnp.sum(weights, axis=2)
    weighted = jnp.einsum(
        "qhk,khd->qhd", weights.astype(jnp.bfloat16), values, preferred_element_type=jnp.float32
    )
    return (new_top, denominator, weighted)


def local(streams, doc_ids, mix_weight, mix_bias, attn_gain, w_qkv, w_out):
    token_rows = streams.shape[0]
    width_local = streams.shape[2]
    heads_local = width_local // HEAD_DIM
    wide_streams = streams.astype(jnp.float32)
    squares = jnp.sum(wide_streams * wide_streams, axis=(1, 2))
    partial_logits = jnp.einsum(
        "tsd,sdc->tc", wide_streams, mix_weight, precision=lax.Precision.HIGHEST
    )
    squares_all, logits_all = packed_total((squares, partial_logits), TP)
    input_weights, output_weights, mixing = coefficients(squares_all, logits_all, mix_bias)
    mixed_input = jnp.einsum(
        "ts,tsd->td", input_weights, wide_streams, precision=lax.Precision.HIGHEST
    ).astype(jnp.bfloat16)
    flat_weight = w_qkv.reshape(w_qkv.shape[0], 3 * width_local)
    piece_wide = gathered_by_axis(mixed_input, TP, 1).astype(jnp.float32)
    gained = (piece_wide * attn_gain).astype(jnp.bfloat16)
    summed = jnp.dot(gained, flat_weight, preferred_element_type=jnp.float32)
    summed, square_sum = (summed, jnp.sum(piece_wide * piece_wide, axis=1))
    norm_scale = lax.rsqrt(square_sum / D + norm_eps)
    projected = (
        (summed * norm_scale[:, None]).astype(jnp.bfloat16).reshape(token_rows, 3, width_local)
    )
    queries = projected[:, 0].reshape(token_rows, heads_local, HEAD_DIM)
    keys_values = projected[:, 1:3]
    seq_index = lax.axis_index("seq")
    query_pos = seq_index * token_rows + jnp.arange(token_rows, dtype=jnp.int32)
    first_doc = doc_ids[0]
    running = (
        jnp.full((token_rows, heads_local), masked_score, jnp.float32),
        jnp.zeros((token_rows, heads_local), jnp.float32),
        jnp.zeros((token_rows, heads_local, HEAD_DIM), jnp.float32),
    )
    piece_kv = lax.all_gather(keys_values, "seq", axis=0, tiled=True)
    piece_doc = lax.all_gather(doc_ids, "seq", axis=0, tiled=True)
    needed = (jnp.int32(0) < (seq_index + 1) * token_rows) & (piece_doc[-1] >= first_doc)
    running = lax.cond(
        needed,
        lambda running_matrix: attend(
            running_matrix, queries, piece_kv, piece_doc, query_pos, doc_ids
        ),
        lambda running_matrix: running_matrix,
        running,
    )
    top_score, denominator, weighted = running
    context = (
        (weighted / denominator[:, :, None]).astype(jnp.bfloat16).reshape(token_rows, width_local)
    )
    branch_out = summed_rows(
        lax.dot_general(
            w_out, context, (((0,), (1,)), ((), ())), preferred_element_type=jnp.float32
        ),
        TP,
    )
    carried = jnp.einsum("tij,tjd->tid", mixing, wide_streams, precision=lax.Precision.HIGHEST)
    return (carried + output_weights[:, :, None] * branch_out.T[:, None, :]).astype(jnp.bfloat16)


def solution(mesh):
    split = Mesh(mesh.devices.reshape(mesh.shape["seq"], 4, 2), ("seq", "tp_0", "tp_1"))
    in_specs = (
        P("seq", None, TP),
        P("seq"),
        P(None, TP, None),
        P(),
        P(),
        P(None, None, TP),
        P(TP, None),
    )
    out_specs = P("seq", None, TP)
    return jax.shard_map(local, mesh=split, in_specs=in_specs, out_specs=out_specs, check_vma=False)
```

profile of v0, /device:TPU:25, one launch (start us, length us, event | category | flops | bytes accessed | tf_op | source)
XLA Modules:
  0.0 438.3 jit_solution(9482599936923689184)
XLA Ops:
  6.5 3.3 multiply_reduce_fusion
  9.9 3.6 fusion.27
  13.9 12.1 %all_to_all.6 = f32[8,1,12800]{2,1,0:T(1,128)S(1)} all-to-all(f32[8,1,12800]{2,1,0:T(1,128)S(1)} %broadcast_in_dim.37), channel_id=1, replica_groups=mesh['seq'=16,'tp_0'=4,'tp_1'=2] {'tp_0','tp_1'}, dimensions={0} | all-to-all | bytes 819200 | tf_op jit(solution)/shard_map/all_to_all | solution.py:20
  26.6 0.7 divide_add_fusion
  27.5 5.3 %fusion.41 = bf16[512,1,512]{2,1,0:T(2,128)(2,1)S(1)} fusion(f32[512,4,1]{1,2,0:T(1,128)S(1)} %copy.89, bf16[512,4,512]{2,1,0:T(4,128)(2,1)} %param.11), kind=kOutput, calls=%fused_computation.53 | convolution fusion | flops 12582912 | bytes 2629632 | tf_op jit(solution)/shard_map/ts,tsd->td/dot_general | solution.py:102
  32.8 0.9 copy.102
  33.8 25.0 %all-gather.5.cloned.1.call-done = bf16[512,1024]{1,0:T(8,128)(2,1)} async-done(((bf16[512,512]{1,0:T(8,128)(2,1)}), bf16[512,1024]{1,0:T(8,128)(2,1)}) %all-gather.5.cloned.1.call-update) | async-done | bytes 1048592 | tf_op jit(solution)/shard_map/all_gather | solution.py:39
  59.1 17.1 %copy.81 = bf16[4096,3,512]{0,2,1:T(8,128)(2,1)} copy(bf16[4096,3,512]{2,0,1:T(8,128)(2,1)} %param.16) | data formatting | bytes 25165824 | tf_op args[5]
  76.2 34.2 %all-gather.7.cloned.1.call-done = bf16[512,4096]{1,0:T(8,128)(2,1)} async-done(((bf16[512,1024]{1,0:T(8,128)(2,1)}), bf16[512,4096]{1,0:T(8,128)(2,1)}) %all-gather.7.cloned.1.call-update) | async-done | bytes 4194320 | tf_op jit(solution)/shard_map/all_gather | solution.py:39
  110.3 3.1 fusion.14
  113.4 11.0 %fusion.22 = bf16[512,1536]{1,0:T(8,128)(2,1)S(1)} fusion(bf16[4096,1536]{0,1:T(8,128)(2,1)} %bitcast.48, bf16[512,4096]{1,0:T(8,128)(2,1)} %all-gather.7.cloned.1.call-done, f32[4096]{0:T(1024)S(1)} %copy-done.5, f32[512]{0:T(512)S(1)} %add_rsqrt_fusion), kind=kOutput, calls=%fused_computation.28 | convolution fusion | flops 6450315264 | bytes 18368512 | tf_op jit(solution)/shard_map/dot_general | solution.py:108
  124.4 0.7 copy.82
  125.1 1.0 slice.48
  126.2 0.5 slice.39
  126.8 23.8 %all-gather = s32[16,1,512]{2,1,0:T(1,128)S(1)} all-gather(s32[1,1,512]{2,1,0:T(1,128)S(1)} %bitcast.58), channel_id=1, replica_groups=mesh['seq'=16,'tp_0'=4,'tp_1'=2] {'seq'}, dimensions={0}, use_global_device_ids=true | all-gather | bytes 34816 | tf_op jit(solution)/shard_map/all_gather | solution.py:125
  150.6 0.6 slice.46
  152.4 91.7 %all-gather.9.cloned.1.call-done = bf16[8192,2,512]{0,2,1:T(8,128)(2,1)} async-done(((bf16[512,2,512]{0,2,1:T(8,128)(2,1)}), bf16[8192,2,512]{0,2,1:T(8,128)(2,1)}) %all-gather.9.cloned.1.call-update) | async-done | bytes 16777232 | tf_op jit(solution)/shard_map/all_gather | solution.py:124
  244.1 103.6 %conditional.1 = (f32[512,4]{0,1:T(4,128)S(1)}, f32[512,4,128]{0,2,1:T(8,128)S(1)}) conditional(s32[]{:T(128)} %convert_element_type.35, () %tuple.18, (s32[]{:T(128)}, s32[512]{0:T(512)S(1)}, s32[8192]{0:T(1024)S(1)}, s32[512]{0:T(512)S(1)}, bf16[8192,2,512]{0,2,1:T(8,128)(2,1)}, /*index=5*/bf16[512,3,512]{0,2,1:T(8,128)(2,1)S(1)}) %tuple.51), branch_computations={%region_7.0_spmd, %region_8.11_spmd} | conditional | flops 8820619264 | bytes 290021440 | solution.py:127
  244.1 4.4 %fusion.6 = pred[512,8192]{0,1:T(8,128)(4,1)S(1)} fusion(s32[512]{0:T(512)S(1)} %get-tuple-element.37, s32[512]{0:T(512)S(1)} %broadcast_add_fusion, s32[8192]{0:T(1024)S(1)} %get-tuple-element.36), kind=kLoop, calls=%fused_computation.10 | loop fusion | flops 12582912 | bytes 4231168 | tf_op jit(solution)/shard_map/cond/branch_1_fun/and | solution.py:78
  248.5 13.1 %fusion.40 = (bf16[8192,1,512]{0,2,1:T(8,128)(2,1)}, bf16[8192,1,512]{0,2,1:T(8,128)(2,1)}) fusion(bf16[8192,2,512]{0,2,1:T(8,128)(2,1)} %get-tuple-element.38), kind=kLoop, calls=%fused_computation.52 | loop fusion | bytes 33554432 | tf_op jit(solution)/shard_map/cond/branch_1_fun/slice | solution.py:73
  261.7 27.6 %fusion = (f32[512,4]{0,1:T(4,128)S(1)}, f32[4,8192,512]{2,1,0:T(8,128)}) fusion(pred[512,8192]{0,1:T(8,128)(4,1)S(1)} %fusion.6, bf16[8192,4,128]{0,2,1:T(8,128)(2,1)} %bitcast.50, bf16[512,4,128]{0,2,1:T(8,128)(2,1)S(1)} %bitcast.55), kind=kOutput, calls=%fused_computation.4 | convolution fusion | flops 4345296896 | bytes 80224256 | tf_op jit(solution)/shard_map/cond/branch_1_fun/qhd,khd->qhk/dot_general | solution.py:74
  289.3 35.2 %fusion.7 = f32[512,4,128]{2,0,1:T(8,128)S(1)} fusion(bf16[8192,4,128]{0,2,1:T(8,128)(2,1)} %bitcast.49, f32[4,8192,512]{2,1,0:T(8,128)} %get-tuple-element.56, f32[512,4]{0,1:T(4,128)S(1)} %broadcast_maximum_fusion, pred[512,8192]{0,1:T(8,128)(4,1)} %copy-done.2), kind=kOutput, calls=%fused_computation.11 | convolution fusion | flops 4378853376 | bytes 80748544 | tf_op jit(solution)/shard_map/cond/branch_1_fun/qhk,khd->qhd/dot_general | solution.py:85
  324.5 0.3 copy.93
  324.9 22.9 %fusion.2 = f32[512,4]{0,1:T(4,128)S(1)} fusion(f32[4,8192,512]{2,1,0:T(8,128)} %get-tuple-element.56, f32[512,4]{0,1:T(4,128)S(1)} %broadcast_maximum_fusion, pred[512,8192]{0,1:T(8,128)(4,1)} %copy-done.2), kind=kLoop, calls=%fused_computation.6 | loop fusion | flops 83884032 | bytes 71319552 | tf_op jit(solution)/shard_map/cond/branch_1_fun/reduce_sum | solution.py:84
  347.9 6.6 %fusion.15 = bf16[4096,512]{0,1:T(8,128)(2,1)} fusion(bf16[512,512]{0,1:T(8,128)(2,1)S(1)} %bitcast.53, bf16[512,4096]{1,0:T(8,128)(2,1)} %param.17), kind=kOutput, calls=%fused_computation.22 | convolution fusion | flops 2149580800 | bytes 8912896 | tf_op jit(solution)/shard_map/dot_general | solution.py:140
  354.9 44.8 %reduce-scatter.3.cloned.1.call-done = bf16[1024,512]{0,1:T(8,128)(2,1)} async-done(((bf16[4096,512]{0,1:T(8,128)(2,1)}), bf16[1024,512]{0,1:T(8,128)(2,1)}) %reduce-scatter.3.cloned.1.call-update) | async-done | bytes 1048592 | tf_op jit(solution)/shard_map/reduce_scatter | solution.py:46
  399.6 2.1 while.10
  401.8 0.9 copy.80
  402.6 0.4 copy.79
  403.1 20.7 %reduce-scatter.5.cloned.1.call-done = bf16[512,512]{0,1:T(8,128)(2,1)} async-done(((bf16[1024,512]{0,1:T(8,128)(2,1)}), bf16[512,512]{0,1:T(8,128)(2,1)}) %reduce-scatter.5.cloned.1.call-update) | async-done | bytes 524304 | tf_op jit(solution)/shard_map/reduce_scatter | solution.py:46
  423.8 1.2 convert_bitcast_fusion
  424.9 6.9 %add_convert_fusion = bf16[512,4,512]{2,1,0:T(4,128)(2,1)} fusion(f32[512,4,4]{2,1,0:T(4,128)S(1)} %copy.79, bf16[512,4,512]{2,1,0:T(4,128)(2,1)S(1)} %copy-done.3, f32[512,512]{1,0:T(8,128)S(1)} %convert_bitcast_fusion, f32[512,4]{1,0:T(8,128)} %copy.80), kind=kOutput, calls=%fused_computation.24 | convolution fusion | flops 53477376 | bytes 5283840 | tf_op jit(solution)/shard_map/tij,tjd->tid/dot_general | solution.py:145
  (100 shorter events, 3.7 us)
Async XLA Ops:
  6.5 3.3 copy-start
  6.5 52.3 %all-gather.5.cloned.1.call-start = ((), (), s32[]{:S(2)}) async-start(), calls=%async_computation.3 | async-start | bytes 1572864 | tf_op jit(solution)/shard_map/all_gather | solution.py:39
  33.8 76.5 %all-gather.7.cloned.1.call-start = ((), (), s32[]{:S(2)}) async-start(), calls=%async_computation.4 | async-start | bytes 5242880 | tf_op jit(solution)/shard_map/all_gather | solution.py:39
  58.9 54.6 %copy-start.5 = (f32[4096]{0:T(1024)S(1)}, f32[4096]{0:T(1024)}, u32[]{:S(2)}) copy-start(f32[4096]{0:T(1024)} %param.15) | copy-start | bytes 49156
  58.9 185.2 %all-gather.9.cloned.1.call-start = ((), (), s32[]{:S(2)}) async-start(), calls=%async_computation.5 | async-start | bytes 17825792 | tf_op jit(solution)/shard_map/all_gather | solution.py:124
  113.4 12.8 %copy-start.4 = (s32[512]{0:T(512)S(1)}, s32[512]{0:T(512)}, u32[]{:S(2)}) copy-start(s32[512]{0:T(512)} %param.12) | copy-start | bytes 6148
  126.2 273.4 %reduce-scatter.3.cloned.1.call-start = ((), (), s32[]{:S(2)}) async-start(), calls=%async_computation.6 | async-start | bytes 5242880 | tf_op jit(solution)/shard_map/reduce_scatter | solution.py:46
  248.5 13.2 %copy-start.2 = (pred[512,8192]{0,1:T(8,128)(4,1)}, pred[512,8192]{0,1:T(8,128)(4,1)S(1)}, u32[]{:S(2)}) copy-start(pred[512,8192]{0,1:T(8,128)(4,1)S(1)} %fusion.6) | copy-start | bytes 12582916 | tf_op jit(solution)/shard_map/cond
  347.9 77.1 %copy-start.3 = (bf16[512,4,512]{2,1,0:T(4,128)(2,1)S(1)}, bf16[512,4,512]{2,1,0:T(4,128)(2,1)}, u32[]{:S(2)}) copy-start(bf16[512,4,512]{2,1,0:T(4,128)(2,1)} %param.11) | copy-start | bytes 6291460
  354.5 77.3 %copy-start.1 = (f32[4,512,24]{1,2,0:T(8,128)S(1)}, f32[4,512,24]{1,2,0:T(8,128)}, u32[]{:S(2)}) copy-start(f32[4,512,24]{1,2,0:T(8,128)} %param.13) | copy-start | bytes 589828
  354.6 69.2 %reduce-scatter.5.cloned.1.call-start = ((), (), s32[]{:S(2)}) async-start(), calls=%async_computation.7 | async-start | bytes 1572864 | tf_op jit(solution)/shard_map/reduce_scatter | solution.py:46
Sparse Core Ops, SparseCore 0:
  33.9 24.8 all-gather.4
  60.5 49.7 all-gather.6
  126.3 117.7 all-gather.8
  354.7 44.8 reduce-scatter.2
  401.8 21.9 reduce-scatter.4
where the time goes:
time: 441 us; the launch traced here: 438 us
  waiting for transfers between devices  216 us (49%)
  matrix products  96.2 us (22%)
  other arithmetic  37.8 us (9%)
  local copies, waits for them, and re-layouts  36.5 us (8%)
  blocking collectives  35.9 us (8%)
  between operations  14.6 us (3%)
    all_gather x1, waiting for transfers between devices, local(): piece_kv = lax.all_gather(keys_values, 'seq', axis=0, tiled=True)  91.7 us
    reduce_scatter x2, waiting for transfers between devices, summed_rows(): subtotal = lax.psum_scatter(subtotal, axis, scatter_dimension=0, tiled=True)  65.4 us
    all_gather x2, waiting for transfers between devices, gathered_by_axis(): nearer = lax.all_gather(x, axes[-1], axis=dim, tiled=True)  59.2 us
    dot_general x1, matrix products, attend(): jnp.einsum('qhk,khd->qhd', weights.astype(jnp.bfloat16), values, preferre...  35.2 us
    dot_general x1, matrix products, attend(): jnp.einsum('qhd,khd->qhk', queries, keys, preferred_element_type=jnp.floa...  27.6 us
    all_gather x1, blocking collectives, local(): piece_doc = lax.all_gather(doc_ids, 'seq', axis=0, tiled=True)  23.8 us
    reduce_sum x1, other arithmetic, attend(): denominator = jnp.sum(weights, axis=2)  22.9 us
    unnamed x11, local copies, waits for them, and re-layouts  17.1 us
  transfers between devices with their start and end apart: 5, of which 5 were waited for; matrix products, arithmetic and copies ran while one was open for 5% of the time, Pallas kernels for 0%

commit v1 on v0

v1 whole, which is shorter than its diff:
```python
import jax
import jax.numpy as jnp
from jax import lax
from jax.experimental import pallas as pl
from jax.experimental.pallas import tpu as pltpu
from jax.sharding import PartitionSpec as P

D = 4096
HD = 128
S = 4
ROUNDS = 20
EPS = 1e-6
T = 512
W = 512
NC = 4
R = T // NC
F32 = jnp.float32
BF = jnp.bfloat16
MESH = pl.DeviceIdType.MESH
NT = (((1,), (1,)), ((), ()))
NEG = -1e30
VMEM = pltpu.VMEM
DMA = pltpu.SemaphoreType.DMA


def where_am_i():
    seq = lax.axis_index("seq")
    tp = lax.axis_index("tp")
    return seq, tp


def remote(src, dst, ssem, rsem, seq, tp):
    return pltpu.make_async_remote_copy(
        src_ref=src, dst_ref=dst, send_sem=ssem, recv_sem=rsem,
        device_id={"seq": seq, "tp": tp}, device_id_type=MESH,
    )


def greet(peers):
    barrier = pltpu.get_barrier_semaphore()
    for seq, tp in peers:
        pl.semaphore_signal(barrier, inc=1, device_id={"seq": seq, "tp": tp}, device_id_type=MESH)
    return lambda: pl.semaphore_wait(barrier, len(peers))


def columns(rows8):
    k = rows8.shape[0]
    if k < 128:
        rows8 = jnp.concatenate([rows8, jnp.zeros((128 - k, rows8.shape[1]), F32)], axis=0)
    return rows8.T


def balanced(e0, e1):
    sub = lax.broadcasted_iota(jnp.int32, e0.shape, 0)
    even, low = sub % 2 == 0, sub % 4 < 2

    def row_total(e):
        u = e + jnp.where(even, pltpu.roll(e, 7, 0), pltpu.roll(e, 1, 0))
        return u + jnp.where(low, pltpu.roll(u, 6, 0), pltpu.roll(u, 2, 0))

    def one_round(_, pair):
        e0, e1 = pair
        e0 = e0 / row_total(e0)
        e1 = e1 / row_total(e1)
        t = e0 + e1
        t = t + pltpu.roll(t, 4, 0)
        return e0 / t, e1 / t

    return lax.fori_loop(0, ROUNDS, one_round, (e0, e1))


def first_kernel(
    xs, docs, wmix, bias, gain, w_hbm,
    att, mix_cols, counts,
    wbuf, g, sb, relay, gained, unow, urecv, nall, nrecv, crecv, csend, pre_cols,
    w_sem, u_ss, u_rs, n_ss, n_rs, c_ss, c_rs, g_ss, g_rs, a_ss, a_rs,
    sib_ss, sib_rs, x_ss, x_rs, f_ss, f_rs, sib2_ss, sib2_rs,
):
    seq, tp = where_am_i()
    yhi, z, core = seq // 8, (seq // 2) % 4, seq % 2
    x, y = tp // 2, tp % 2
    tp_peers = [(seq, (tp + r) % 8) for r in range(1, 8)]
    seq_peers = [((seq + r) % 16, tp) for r in range(1, 16)]
    other_y = x * 2 + 1 - y
    diagonal = ((seq + 8) % 16, other_y)
    entered = greet(tp_peers + seq_peers + [diagonal])

    def wcopy(i):
        return pltpu.make_async_copy(w_hbm.at[i], wbuf.at[i], w_sem.at[i])

    for i in range(3):
        wcopy(i).start()

    acc = jnp.zeros((T, 128), F32)
    logits = jnp.zeros((32, T), F32)
    for s in range(S):
        xv = xs[s]
        w = jnp.concatenate([wmix[s], jnp.zeros((8, W), F32)], axis=0)
        hi = w.astype(BF).astype(F32)
        mid = (w - hi).astype(BF).astype(F32)
        low = (w - hi) - mid
        parts = jnp.concatenate([hi, mid, low], axis=0).astype(BF)
        got = lax.dot_general(parts, xv, NT, preferred_element_type=F32)
        logits = logits + (got[0:32] + (got[32:64] + got[64:96]))
        x32 = xv.astype(F32)
        sq = x32 * x32
        acc = acc + ((sq[:, 0:128] + sq[:, 128:256]) + (sq[:, 256:384] + sq[:, 384:512]))
    squares = jnp.sum(acc.T, axis=0, keepdims=True)
    sub = lax.broadcasted_iota(jnp.int32, (8, T), 0)
    unow[...] = jnp.where(sub < 4, logits[0:8], jnp.where(sub == 4, jnp.broadcast_to(squares, (8, T)), 0.0))
    nall[...] = logits[0:24]
    dv = docs[...]
    csub = lax.broadcasted_iota(jnp.int32, (8, 128), 0)
    cv = jnp.zeros((8, 128), jnp.int32)
    for k in range(1, 4):
        n = jnp.sum(jnp.where(dv < k, 1, 0), axis=1, keepdims=True)
        n = jnp.sum(n, axis=0, keepdims=True)
        cv = jnp.where(csub == k, jnp.broadcast_to(n, (8, 128)), cv)
    csend[...] = cv

    entered()
    for r, (sq_, tp_) in enumerate(tp_peers):
        remote(unow, urecv.at[r], u_ss.at[r], u_rs.at[r], sq_, tp_).start()
    for r, (sq_, tp_) in enumerate(seq_peers):
        remote(csend, crecv.at[r], c_ss.at[r], c_rs.at[r], sq_, tp_).start()

    total = unow[...]
    for r, (sq_, tp_) in enumerate(tp_peers):
        remote(unow, urecv.at[r], u_ss.at[r], u_rs.at[r], sq_, tp_).wait_recv()
        total = total + urecv[r]
    inv_rms = lax.rsqrt(total[4:5] / (S * D) + EPS)
    pre = 1.0 / (1.0 + jnp.exp(-(total * inv_rms + bias[0:8])))
    pre_cols[...] = columns(pre)

    right = ((x + 1) % 4) * 2 + y
    left = ((x + 3) % 4) * 2 + y
    b_p = other_y
    b_l0, b_l1 = left, ((x + 3) % 4) * 2 + 1 - y
    b_r0, b_r1 = right, ((x + 1) % 4) * 2 + 1 - y
    b_f0, b_f1 = ((x + 2) % 4) * 2 + y, ((x + 2) % 4) * 2 + 1 - y

    def move(c, k, blk, role, to):
        return remote(g.at[c, blk], g.at[c, blk], g_ss.at[c, k], g_rs.at[c, role], seq, to)

    def arrived(c, role, blk):
        move(c, 0, blk, role, right).wait_recv()

    def make_chunk(c):
        rows = slice(c * R, (c + 1) * R)
        v = pre_cols[rows, 0:1] * xs[0, rows, :].astype(F32)
        for s in range(1, S):
            v = v + pre_cols[rows, s : s + 1] * xs[s, rows, :].astype(F32)
        g[c, tp] = v.astype(BF)

    def send_chunk(c):
        move(c, 0, tp, 1, right).start()
        move(c, 1, tp, 3, left).start()
        move(c, 2, tp, 0, other_y).start()

    make_chunk(0)
    for c in range(NC):
        if c + 1 < NC:
            make_chunk(c + 1)
        send_chunk(c)
    for c in range(NC):
        arrived(c, 0, b_p)
        move(c, 3, b_p, 2, right).start()
        move(c, 4, b_p, 4, left).start()
        arrived(c, 1, b_l0)
        move(c, 5, b_l0, 5, right).start()
        arrived(c, 4, b_r1)
        move(c, 6, b_r1, 6, left).start()
    for r, (sq_, tp_) in enumerate(tp_peers):
        remote(nall, nrecv.at[r], n_ss.at[r], n_rs.at[r], sq_, tp_).start()
    for i in range(3):
        wcopy(i).wait()

    def block_of(half, d):
        return half * 8 + ((z + 4 - d) % 4) * 2 + core

    def spread(c, d):
        to_z = (z + d) % 4
        return remote(
            sb.at[to_z, c], att.at[seq, c], a_ss.at[c, d - 1], a_rs.at[c, d - 1],
            yhi * 8 + to_z * 2 + core, tp,
        )

    def twin(c, d):
        ref = att.at[block_of(yhi, d), c, pl.ds(0, 2)]
        return remote(ref, ref, sib_ss.at[c, d], sib_rs.at[c, d], seq + 1 - 2 * core, tp)

    def twin_in(c, d):
        ref = att.at[yhi * 8 + ((z + 4 - d) % 4) * 2 + 1 - core, c, pl.ds(0, 2)]
        return remote(ref, ref, sib_ss.at[c, d], sib_rs.at[c, d], seq + 1 - 2 * core, tp)

    def cross(c, d):
        ref = att.at[block_of(0, d), c, pl.ds(0, 2)]
        return remote(ref, relay.at[d, c], x_ss.at[c, d], x_rs.at[c, d], diagonal[0], diagonal[1])

    def final(c, d):
        return remote(
            relay.at[d, c], att.at[block_of(0, d), c, pl.ds(0, 2)],
            f_ss.at[c, d], f_rs.at[c, d], seq, other_y,
        )

    def twin2(c, d):
        ref = att.at[block_of(0, d), c, pl.ds(0, 2)]
        return remote(ref, ref, sib2_ss.at[c, d], sib2_rs.at[c, d], seq + 1 - 2 * core, tp)

    def twin2_in(c, d):
        ref = att.at[((z + 4 - d) % 4) * 2 + 1 - core, c, pl.ds(0, 2)]
        return remote(ref, ref, sib2_ss.at[c, d], sib2_rs.at[c, d], seq + 1 - 2 * core, tp)

    def step(c, carry):
        @pl.when(c < NC)
        def _():
            arrived(c, 2, b_l1)
            arrived(c, 3, b_r0)
            arrived(c, 5, b_f0)
            arrived(c, 6, b_f1)
            ss = jnp.zeros((R, 128), F32)
            for b in range(8):
                g32 = g[c, b].astype(F32)
                q = g32 * g32
                ss = ss + ((q[:, 0:128] + q[:, 128:256]) + (q[:, 256:384] + q[:, 384:512]))
                gained[:, b * W : (b + 1) * W] = (g32 * gain[:, b * W : (b + 1) * W]).astype(BF)
            norm = lax.rsqrt(jnp.sum(ss, axis=1, keepdims=True) / D + EPS)
            lhs = gained[...]
            for slot, third in ((0, 1), (1, 2), (2, 0)):
                acc = jnp.dot(lhs, wbuf[third], preferred_element_type=F32)
                out = (acc * norm).astype(BF)
                for h in range(4):
                    sb[h, c, slot] = out[:, h * HD : (h + 1) * HD]
            att[seq, c] = sb[z, c]
            for d in (2, 1, 3):
                spread(c, d).start()

        @pl.when((c >= 1) & (c <= NC))
        def _():
            for d in range(4):
                if d:
                    spread_in(c - 1, d)
                twin(c - 1, d).start()

                @pl.when(yhi == 0)
                def _():
                    cross(c - 1, d).start()

        @pl.when((c >= 2) & (c <= NC + 1) & (yhi == 1))
        def _():
            for d in range(4):
                cross(c - 2, d).wait_recv()
                final(c - 2, d).start()

        @pl.when((c >= 3) & (yhi == 1))
        def _():
            for d in range(4):
                final(c - 3, d).wait_recv()
                twin2(c - 3, d).start()

        return carry

    def spread_in(c, d):
        ref = att.at[block_of(yhi, d), c]
        remote(sb.at[z, c], ref, a_ss.at[c, d - 1], a_rs.at[c, d - 1], seq, other_y).wait_recv()

    lax.fori_loop(0, NC + 3, step, 0)

    ztot = nall[...]
    for r, (sq_, tp_) in enumerate(tp_peers):
        remote(nall, nrecv.at[r], n_ss.at[r], n_rs.at[r], sq_, tp_).wait_recv()
        ztot = ztot + nrecv[r]
    ztot = ztot * inv_rms + bias[...]
    post = 2.0 / (1.0 + jnp.exp(-ztot[0:8]))
    e0, e1 = balanced(jnp.exp(ztot[8:16]), jnp.exp(ztot[16:24]))
    mix_cols[...] = columns(jnp.concatenate([post, e0, e1], axis=0))
    cv = csend[...]
    for r, (sq_, tp_) in enumerate(seq_peers):
        remote(csend, crecv.at[r], c_ss.at[r], c_rs.at[r], sq_, tp_).wait_recv()
        cv = cv + crecv[r]
    counts[...] = cv

    for r, (sq_, tp_) in enumerate(tp_peers):
        remote(unow, urecv.at[r], u_ss.at[r], u_rs.at[r], sq_, tp_).wait_send()
        remote(nall, nrecv.at[r], n_ss.at[r], n_rs.at[r], sq_, tp_).wait_send()
    for r, (sq_, tp_) in enumerate(seq_peers):
        remote(csend, crecv.at[r], c_ss.at[r], c_rs.at[r], sq_, tp_).wait_send()

    def drain(c, carry):
        for k in range(7):
            move(c, k, tp, 0, right).wait_send()
        for d in range(1, 4):
            spread(c, d).wait_send()
        for d in range(4):
            twin(c, d).wait_send()
            twin_in(c, d).wait_recv()

        @pl.when(yhi == 0)
        def _():
            for d in range(4):
                cross(c, d).wait_send()

        @pl.when(yhi == 1)
        def _():
            for d in range(4):
                final(c, d).wait_send()
                twin2(c, d).wait_send()
                twin2_in(c, d).wait_recv()

        return carry

    lax.fori_loop(0, NC, drain, 0)


def attention_kernel(att, cnt, ctx, m_ref, l_ref, acc_ref):
    seq, _ = where_am_i()
    yhi, core = seq // 8, seq % 2
    starts = [cnt[k, 0] for k in range(1, 4)]
    scale = HD ** (-0.5) * 1.4426950408889634

    def start_of(p):
        v = p * 0
        for c in starts:
            v = jnp.where(c <= p, jnp.maximum(v, c), v)
        return v

    def one_query_block(qi, carry):
        qb = yhi * 8 + qi * 2 + core
        q = att[qb, :, 2].reshape(T, HD)
        first = start_of(qb * T)
        last = start_of(qb * T + T - 1)
        lo = first // T
        mid = jnp.minimum((last + T - 1) // T, qb)
        qpos = qb * T + lax.broadcasted_iota(jnp.int32, (T, 1), 0)
        qstart = start_of(qpos)
        m_ref[...] = jnp.full((T, 128), NEG, F32)
        l_ref[...] = jnp.zeros((T, 128), F32)
        acc_ref[...] = jnp.zeros((T, HD), F32)

        def block(kb, masked):
            k = att[kb, :, 0].reshape(T, HD)
            v = att[kb, :, 1].reshape(T, HD)
            s = lax.dot_general(q, k, NT, preferred_element_type=F32)
            if masked:
                kpos = kb * T + lax.broadcasted_iota(jnp.int32, (1, T), 1)
                ok = (kpos <= qpos) & (kpos >= qstart)
                s = jnp.where(ok, s, NEG)
            top = jnp.maximum(
                jnp.maximum(s[:, 0:128], s[:, 128:256]), jnp.maximum(s[:, 256:384], s[:, 384:512])
            )
            m_old = m_ref[:, 0:1]
            m_new = jnp.maximum(m_old, jnp.max(top, axis=1, keepdims=True))
            p = jnp.exp2((s - m_new) * scale)
            if masked:
                p = jnp.where(ok, p, 0.0)
            alpha = jnp.exp2((m_old - m_new) * scale)
            part = (p[:, 0:128] + p[:, 128:256]) + (p[:, 256:384] + p[:, 384:512])
            l_ref[...] = l_ref[...] * alpha + part
            acc_ref[...] = acc_ref[...] * alpha + jnp.dot(p.astype(BF), v, preferred_element_type=F32)
            m_ref[...] = jnp.broadcast_to(m_new, (T, 128))

        def with_mask(kb, c):
            block(kb, True)
            return c

        def without(kb, c):
            block(kb, False)
            return c

        lax.fori_loop(lo, mid, with_mask, 0)
        lax.fori_loop(mid, qb, without, 0)
        lax.fori_loop(qb, qb + 1, with_mask, 0)
        out = acc_ref[...] / jnp.sum(l_ref[...], axis=1, keepdims=True)
        ctx[qi] = out.astype(BF).reshape(NC, R, HD)
        return carry

    lax.fori_loop(0, 4, one_query_block, 0)


def last_kernel(
    ctx, mix_cols, xs, w_hbm,
    out,
    wbuf, cbuf, snd, own, rcv,
    w_sem, z_ss, z_rs, s_ss, s_rs,
):
    seq, tp = where_am_i()
    yhi, z, core = seq // 8, (seq // 2) % 4, seq % 2
    x, y = tp // 2, tp % 2
    right = ((x + 1) % 4) * 2 + y
    left = ((x + 3) % 4) * 2 + y
    other_y = x * 2 + 1 - y
    z_peers = [yhi * 8 + ((z + d) % 4) * 2 + core for d in range(1, 4)]
    entered = greet([(p, tp) for p in z_peers] + [(seq, right), (seq, left), (seq, other_y)])
    wcopy = pltpu.make_async_copy(w_hbm, wbuf, w_sem)
    wcopy.start()
    entered()

    def back(c, d):
        to_z = (z + d) % 4
        return remote(
            ctx.at[to_z, c], cbuf.at[z, c], z_ss.at[c, d - 1], z_rs.at[c, d - 1], z_peers[d - 1], tp
        )

    def back_in(c, d):
        from_z = (z + 4 - d) % 4
        remote(
            ctx.at[z, c], cbuf.at[from_z, c], z_ss.at[c, d - 1], z_rs.at[c, d - 1], z_peers[d - 1], tp
        ).wait_recv()

    for c in range(NC):
        for d in (2, 1, 3):
            back(c, d).start()
    cbuf[z] = ctx[z]
    wcopy.wait()

    def pass_on(c, k, to):
        return remote(snd.at[c, k], rcv.at[c, k], s_ss.at[c, k], s_rs.at[c, k], seq, to)

    b0, b1 = ((x + 1) % 4) * 2, ((x + 3) % 4) * 2
    bf = ((x + 2) % 4) * 2

    def project(c, carry):
        for d in range(1, 4):
            back_in(c, d)
        lhs = jnp.concatenate([cbuf[h, c] for h in range(4)], axis=1)

        def term(b):
            cols = pl.ds(pl.multiple_of(b * W, W), W)
            return jnp.dot(lhs, wbuf[:, cols], preferred_element_type=F32)

        snd[c, 0] = term(bf).astype(BF)
        snd[c, 1] = term(bf + 1).astype(BF)
        pass_on(c, 0, right).start()
        pass_on(c, 1, left).start()
        snd[c, 3] = term(b0 + 1).astype(BF)
        snd[c, 4] = term(b1).astype(BF)
        pass_on(c, 3, right).start()
        pass_on(c, 4, left).start()
        own[c, 0] = term(b0)
        own[c, 1] = term(b1 + 1)
        own[c, 2] = term(x * 2)
        own[c, 3] = term(x * 2 + 1)
        return carry

    lax.fori_loop(0, NC, project, 0)

    def second(c, carry):
        pass_on(c, 0, right).wait_recv()
        snd[c, 2] = (own[c, 0] + rcv[c, 0].astype(F32)).astype(BF)
        pass_on(c, 2, right).start()
        pass_on(c, 1, left).wait_recv()
        snd[c, 5] = (own[c, 1] + rcv[c, 1].astype(F32)).astype(BF)
        pass_on(c, 5, left).start()
        return carry

    lax.fori_loop(0, NC, second, 0)

    def third(c, carry):
        @pl.when(c < NC)
        def _():
            for k in (3, 4, 2, 5):
                pass_on(c, k, right).wait_recv()
            o = 1 - y
            snd[c, 6] = (
                own[c, 2 + o] + rcv[c, 2 + o].astype(F32) + rcv[c, 4 + o].astype(F32)
            ).astype(BF)
            pass_on(c, 6, other_y).start()

        @pl.when(c >= 1)
        def _():
            e = c - 1
            pass_on(e, 6, other_y).wait_recv()
            rows = pl.ds(pl.multiple_of(e * R, R), R)
            branch = (own[e, 2 + y] + rcv[e, 2 + y].astype(F32)) + (
                rcv[e, 4 + y].astype(F32) + rcv[e, 6].astype(F32)
            )
            wide = [xs[j, rows, :].astype(F32) for j in range(S)]
            for i in range(S):
                v = mix_cols[rows, 4 + i : 5 + i] * branch
                for j in range(S):
                    k = 8 + 4 * i + j
                    v = v + mix_cols[rows, k : k + 1] * wide[j]
                out[i, rows, :] = v.astype(BF)

        return carry

    lax.fori_loop(0, NC + 1, third, 0)

    def drain(c, carry):
        for d in range(1, 4):
            back(c, d).wait_send()
        for k in range(7):
            pass_on(c, k, right).wait_send()
        return carry

    lax.fori_loop(0, NC, drain, 0)


def local(streams, doc_ids, mix_weight, mix_bias, attn_gain, w_qkv, w_out):
    xs = jnp.transpose(streams, (1, 0, 2))
    wmix = jnp.transpose(mix_weight, (0, 2, 1))
    wq = jnp.transpose(w_qkv, (1, 0, 2))
    vm = pl.BlockSpec(memory_space=VMEM)
    hbm = pl.BlockSpec(memory_space=pl.ANY)
    sds = jax.ShapeDtypeStruct
    att, mix_cols, counts = pl.pallas_call(
        first_kernel,
        name="gather_project",
        out_shape=(
            sds((16, NC, 3, R, HD), BF),
            sds((T, 128), F32),
            sds((8, 128), jnp.int32),
        ),
        in_specs=[vm, vm, vm, vm, vm, hbm],
        out_specs=(vm, vm, vm),
        scratch_shapes=[
            VMEM((3, D, W), BF),
            VMEM((NC, 8, R, W), BF),
            VMEM((4, NC, 3, R, HD), BF),
            VMEM((4, NC, 2, R, HD), BF),
            VMEM((R, D), BF),
            VMEM((8, T), F32),
            VMEM((7, 8, T), F32),
            VMEM((24, T), F32),
            VMEM((7, 24, T), F32),
            VMEM((15, 8, 128), jnp.int32),
            VMEM((8, 128), jnp.int32),
            VMEM((T, 128), F32),
            DMA((3,)),
            DMA((7,)), DMA((7,)),
            DMA((7,)), DMA((7,)),
            DMA((15,)), DMA((15,)),
            DMA((NC, 7)), DMA((NC, 7)),
            DMA((NC, 3)), DMA((NC, 3)),
            DMA((NC, 4)), DMA((NC, 4)),
            DMA((NC, 4)), DMA((NC, 4)),
            DMA((NC, 4)), DMA((NC, 4)),
            DMA((NC, 4)), DMA((NC, 4)),
        ],
        compiler_params=pltpu.CompilerParams(
            collective_id=0, has_side_effects=True, vmem_limit_bytes=56 * 1024 * 1024
        ),
    )(
        xs, doc_ids.reshape(4, 128), wmix, mix_bias.reshape(24, 1),
        attn_gain.reshape(1, D), wq,
    )
    ctx = pl.pallas_call(
        attention_kernel,
        name="attention",
        out_shape=sds((4, NC, R, HD), BF),
        in_specs=[vm, pl.BlockSpec(memory_space=pltpu.SMEM)],
        out_specs=vm,
        scratch_shapes=[VMEM((T, 128), F32), VMEM((T, 128), F32), VMEM((T, HD), F32)],
        compiler_params=pltpu.CompilerParams(vmem_limit_bytes=32 * 1024 * 1024),
    )(att, counts)
    out = pl.pallas_call(
        last_kernel,
        name="project_out",
        out_shape=sds((S, T, W), BF),
        in_specs=[vm, vm, vm, hbm],
        out_specs=vm,
        scratch_shapes=[
            VMEM((W, D), BF),
            VMEM((4, NC, R, HD), BF),
            VMEM((NC, 7, R, W), BF),
            VMEM((NC, 4, R, W), F32),
            VMEM((NC, 7, R, W), BF),
            DMA(()),
            DMA((NC, 3)), DMA((NC, 3)),
            DMA((NC, 7)), DMA((NC, 7)),
        ],
        compiler_params=pltpu.CompilerParams(
            collective_id=1, has_side_effects=True, vmem_limit_bytes=48 * 1024 * 1024
        ),
    )(ctx, mix_cols, xs, w_out)
    return jnp.transpose(out, (1, 0, 2))


def solution(mesh):
    in_specs = (
        P("seq", None, "tp"),
        P("seq"),
        P(None, "tp", None),
        P(),
        P(),
        P(None, None, "tp"),
        P("tp", None),
    )
    return jax.shard_map(
        local, mesh=mesh, in_specs=in_specs, out_specs=P("seq", None, "tp"), check_vma=False
    )
```

time: 441 us -> 164 us (0.37)
  waiting for transfers between devices: 216 us -> 0 us
  Pallas kernels: 0 us -> 154 us
  matrix products: 96.2 us -> 0 us
  other arithmetic: 37.8 us -> 0 us
  blocking collectives: 35.9 us -> 0 us
  local copies, waits for them, and re-layouts: 36.5 us -> 11.1 us
  between operations: 14.6 us -> 0.05 us
    pallas_call x0 -> x3, Pallas kernels: none -> 154 us  [the longest x1 85.1 us: local(): pl.pallas_call(first_kernel, name='gather_project', out_shape=(sds((16, N...]
    all_gather x3 -> x0, waiting for transfers between devices: 151 us -> none  [the longest x1 91.7 us: local(): piece_kv = lax.all_gather(keys_values, 'seq', axis=0, tiled=True)]
    dot_general x7 -> x0, matrix products: 96.2 us -> none  [the longest x1 35.2 us: attend(): jnp.einsum('qhk,khd->qhd', weights.astype(jnp.bfloat16), values, preferre...]
    reduce_scatter x2 -> x0, waiting for transfers between devices: 65.4 us -> none  [summed_rows(): subtotal = lax.psum_scatter(subtotal, axis, scatter_dimension=0, tiled=True)]
    reduce_sum x44 -> x0, other arithmetic: 30.7 us -> none  [the longest x1 22.9 us: attend(): denominator = jnp.sum(weights, axis=2)]
    all_gather x1 -> x0, blocking collectives: 23.8 us -> none  [local(): piece_doc = lax.all_gather(doc_ids, 'seq', axis=0, tiled=True)]
    slice x6 -> x0, local copies, waits for them, and re-layouts: 15.4 us -> none  [the longest x1 13.1 us: attend(): values = keys_values[:, 1].reshape(key_count, heads_local, HEAD_DIM)]
    all_to_all x1 -> x0, blocking collectives: 12.1 us -> none  [from_everyone(): return lax.all_to_all(copies, axis, split_axis=0, concat_axis=0, tiled=True)]
  transfers between devices with their start and end apart: 5 -> 0, of which waited for: 5 -> 0; matrix products, arithmetic and copies ran while one was open for 5% -> 0% of each run, Pallas kernels for 0% -> 0%
where the time goes in v1:
time: 164 us; the launch traced here: 165 us
  Pallas kernels  154 us (94%)
  local copies, waits for them, and re-layouts  11.1 us (7%)
    pallas_call x1, Pallas kernels, local(): pl.pallas_call(first_kernel, name='gather_project', out_shape=(sds((16, N...  85.1 us
    pallas_call x1, Pallas kernels, local(): pl.pallas_call(last_kernel, name='project_out', out_shape=sds((S, T, W),...  46.7 us
    pallas_call x1, Pallas kernels, local(): pl.pallas_call(attention_kernel, name='attention', out_shape=sds((4, NC,...  22 us
    unnamed x9, local copies, waits for them, and re-layouts  6.78 us

profile of v1, /device:TPU:25, one launch (start us, length us, event | category | flops | bytes accessed | tf_op | source)
XLA Modules:
  0.0 164.9 jit_solution(15869470399992154079)
XLA Ops:
  0.0 1.3 copy.9.bias
  1.3 3.3 %copy.12 = bf16[512,4,512]{2,0,1:T(8,128)(2,1)} copy(bf16[512,4,512]{2,1,0:T(4,128)(2,1)} %param.7) | data formatting | bytes 4194304 | tf_op args[0]
  4.6 85.1 %gather_project.1 = (bf16[16,4,3,128,128]{4,3,2,1,0:T(8,128)(2,1)}, f32[512,128]{1,0:T(8,128)}, s32[8,128]{1,0:T(8,128)}) custom-call(bf16[4,512,512]{2,1,0:T(8,128)(2,1)} %bitcast.9, s32[4,128]{1,0:T(4,128)} %bitcast.15, f32[4,24,512]{2,1,0:T(8,128)} %bitcast.13, f32[24,1]{1,0:T(8,128)} %copy.9.bias, f32[1,4096]{1,0:T(1,128)} %bitcast.14, ...), custom_call_target="tpu_custom_call" | custom-call | tf_op jit(solution)/shard_map/gather_project/pallas_call | solution.py:506
  89.8 0.0 copy-start.1
  89.8 2.8 %copy-done.1 = bf16[16,4,3,128,128]{4,3,2,1,0:T(8,128)(2,1)S(1)} copy-done((bf16[16,4,3,128,128]{4,3,2,1,0:T(8,128)(2,1)S(1)}, bf16[16,4,3,128,128]{4,3,2,1,0:T(8,128)(2,1)}, u32[]{:S(2)}) %copy-start.1) | copy-done | bytes 6291480
  92.6 0.0 copy-start.3
  92.6 0.7 copy-done.3
  93.2 0.0 copy-start
  93.2 0.0 copy-start.2
  93.3 22.0 %attention.1.ctx = bf16[4,4,128,128]{3,2,1,0:T(8,128)(2,1)S(1)} custom-call(bf16[16,4,3,128,128]{4,3,2,1,0:T(8,128)(2,1)S(1)} %copy-done.1, s32[8,128]{1,0:T(8,128)S(1)} %copy-done.3), custom_call_target="tpu_custom_call" | custom-call | tf_op jit(solution)/shard_map/attention/pallas_call | solution.py:547
  115.2 0.0 copy-done
  115.2 0.0 copy-done.2
  115.2 46.7 %project_out.1 = bf16[4,512,512]{2,1,0:T(8,128)(2,1)S(1)} custom-call(bf16[4,4,128,128]{3,2,1,0:T(8,128)(2,1)S(1)} %attention.1.ctx, f32[512,128]{1,0:T(8,128)S(1)} %copy-done.2, bf16[4,512,512]{2,1,0:T(8,128)(2,1)S(1)} %bitcast.10, bf16[512,4096]{1,0:T(8,128)(2,1)} %w_hbm.1), custom_call_target="tpu_custom_call" | custom-call | tf_op jit(solution)/shard_map/project_out/pallas_call | solution.py:556
  161.9 2.9 %copy.10 = bf16[512,4,512]{2,1,0:T(4,128)(2,1)} copy(bf16[512,4,512]{2,0,1:T(8,128)(2,1)S(1)} %bitcast.11) | data formatting | bytes 4194304 | tf_op jit(solution)/shard_map/transpose | solution.py:576
Async XLA Ops:
  89.8 2.8 %copy-start.1 = (bf16[16,4,3,128,128]{4,3,2,1,0:T(8,128)(2,1)S(1)}, bf16[16,4,3,128,128]{4,3,2,1,0:T(8,128)(2,1)}, u32[]{:S(2)}) copy-start(bf16[16,4,3,128,128]{4,3,2,1,0:T(8,128)(2,1)} %get-tuple-element.8.att) | copy-start | bytes 18874372
  92.6 0.7 copy-start.3
  93.2 22.0 %copy-start = (bf16[512,4,512]{2,0,1:T(8,128)(2,1)S(1)}, bf16[512,4,512]{2,0,1:T(8,128)(2,1)}, u32[]{:S(2)}) copy-start(bf16[512,4,512]{2,0,1:T(8,128)(2,1)} %copy.12) | copy-start | bytes 6291460
  93.2 22.0 %copy-start.2 = (f32[512,128]{1,0:T(8,128)S(1)}, f32[512,128]{1,0:T(8,128)}, u32[]{:S(2)}) copy-start(f32[512,128]{1,0:T(8,128)} %get-tuple-element.10.mix_cols) | copy-start | bytes 786436
